TPU v7x, 32 devices: a whole 2x2x4 slice. The times are simulated.
32 devices in a mesh: kgrp: 2 (over y), band: 4 (over z), fft: 4 (over x, core).
Axes of the slice: x: 2, y: 2, z: 4, core: 2. Of those that a mesh axis runs over, the one named last changes fastest.
Arguments:
- orbitals: float32 [8, 64, 64, 128], P(('kgrp', 'band'), 'fft'), parts along dimension 0, may hold values from -6 to 6
- partners: float32 [8, 64, 64, 128], P(('kgrp', 'band'), 'fft'), parts along dimension 0, may hold values from -6 to 6
- shift_table: float32 [8, 3], replicated, may hold values from -0.5 to 0.5
- shift_index: int32 [8], P('kgrp'), parts along dimension 0, may hold values from 0 to 7
Outputs:
- potential: float32 [8, 64, 64, 128], P(('kgrp', 'band'), 'fft'), parts along dimension 0
- projector: float32 [8, 64, 64, 128], P(('kgrp', 'band'), 'fft'), parts along dimension 0
There are 2 independent parts, one for each index of `kgrp`. A program takes and returns all parts, laid end to end along the dimension named above; an argument that names none is the same for every part. Nothing has to cross between parts.
All inputs are finite; a program needn't handle non-finite values.
Results may differ from a plain program's by a relative error of at most 0.0001.
Values sent between devices are 32-bit elements; how exact they have to be, the bound alone decides.
No kernel may reach another device: no remote copies, remote signals or barrier semaphores. Data moves between devices by JAX's collectives and lax.ppermute only.
A program may use at most 64 MiB of HBM per device.

v0:
```python
import math

import jax
import jax.numpy as jnp
import numpy as np
from jax import lax
from jax.experimental import pallas as pl
from jax.experimental.pallas import tpu as pltpu
from jax.sharding import PartitionSpec as P

PREC = lax.Precision.HIGH
SCREEN_SQUARE = 0.25
FOUR_PI = 4.0 * math.pi


def lane_table(extent, sign):
    index = np.arange(extent)
    wave = np.exp(sign * 2j * np.pi / extent * (np.outer(index, index) % extent))
    full = np.kron(np.array([[1.0, 1.0], [1.0, -1.0]]), wave)
    return np.block([[full.real, full.imag], [-full.imag, full.real]])


def row_table(half, sign):
    index = np.arange(half)
    wave = np.exp(sign * 2j * np.pi / half * (np.outer(index, index) % half))
    return np.block([[wave.real, -wave.imag], [wave.imag, wave.real]])


def twiddle_table(extent, sign):
    half = extent // 2
    wave = np.exp(sign * 2j * np.pi / extent * np.arange(half))
    wave = np.concatenate(
        [np.ones((half, extent)), np.broadcast_to(wave[:, None], (half, extent))], axis=1
    )
    return jnp.asarray(np.stack([wave.real, wave.imag]), jnp.float32)


def halves(table):
    table = np.asarray(table, np.float32)
    high = table.astype(jnp.bfloat16)
    low = (table - high.astype(np.float32)).astype(jnp.bfloat16)
    return high, low


def stage_tables(extent, sign):
    high, low = halves(lane_table(extent, sign))
    lanes = jnp.stack([jnp.asarray(high), jnp.asarray(low)])
    high, low = halves(row_table(extent // 2, sign))
    rows = jnp.asarray(np.concatenate([high, high, low], axis=1))
    return lanes, rows, twiddle_table(extent, sign)


def split_value(value):
    high = value.astype(jnp.bfloat16)
    low = (value - high.astype(jnp.float32)).astype(jnp.bfloat16)
    return high, low


def dot(left, right):
    return jnp.dot(left, right, preferred_element_type=jnp.float32)


def on_lanes(real, imag, table_ref):
    high, low = split_value(jnp.concatenate([real, imag], axis=1))
    out = dot(high, table_ref[0]) + (dot(low, table_ref[0]) + dot(high, table_ref[1]))
    lanes = real.shape[1]
    return out[:, :lanes], out[:, lanes:]


def on_rows(stacked, table_ref):
    high, low = split_value(stacked)
    return dot(table_ref[...], jnp.concatenate([high, low, high], axis=0))


def unpack(tile):
    half, extent = tile.shape[0] // 2, tile.shape[1] // 2
    top, bottom = tile[:half], tile[half:]
    first = lax.broadcasted_iota(jnp.int32, top.shape, 1) < extent
    real = jnp.where(first, top, pltpu.roll(bottom, extent, 1))
    imag = jnp.where(first, pltpu.roll(top, extent, 1), bottom)
    return real, imag


def pack(real, imag):
    extent = real.shape[1] // 2
    first = lax.broadcasted_iota(jnp.int32, real.shape, 1) < extent
    top = jnp.where(first, real, pltpu.roll(imag, extent, 1))
    bottom = jnp.where(first, pltpu.roll(real, extent, 1), imag)
    return top, bottom


def forward_kernel(orb_ref, part_ref, lanes_ref, rows_ref, twid_ref, out_ref):
    count, extent = orb_ref.shape[1], orb_ref.shape[2]
    half = extent // 2
    devices, share = out_ref.shape[0], out_ref.shape[5]
    reals, imags = [], []
    for x in range(count):
        orb_real, orb_imag = unpack(orb_ref[0, x])
        part_real, part_imag = unpack(part_ref[0, x])
        reals.append(part_real * orb_real + part_imag * orb_imag)
        imags.append(part_real * orb_imag - part_imag * orb_real)
    real, imag = on_lanes(jnp.concatenate(reals, 0), jnp.concatenate(imags, 0), lanes_ref)
    cosine, sine = twid_ref[0], twid_ref[1]
    for x in range(0, count, 2):
        pair = []
        for at in (x, x + 1):
            re, im = real[at * half : (at + 1) * half], imag[at * half : (at + 1) * half]
            pair.append(
                jnp.concatenate([re * cosine - im * sine, re * sine + im * cosine], axis=0)
            )
        done = on_rows(jnp.concatenate(pair, axis=1), rows_ref)
        for at in (0, 1):
            piece = done[:, at * 2 * extent : (at + 1) * 2 * extent]
            for device in range(devices):
                lo = device * share
                out_ref[device, 0, 0, 0, x + at] = piece[lo : lo + share]
                out_ref[device, 0, 0, 1, x + at] = piece[half + lo : half + lo + share]


def inverse_kernel(spec_ref, part_ref, *refs, chained):
    prior_ref = refs[0] if chained else None
    lanes_ref, rows_ref, twid_ref, out_ref = refs[-4:]
    count, extent = part_ref.shape[1], part_ref.shape[2]
    half = extent // 2
    devices = spec_ref.shape[0]
    cosine, sine = twid_ref[0], twid_ref[1]
    reals, imags = [], []
    for x in range(0, count, 2):
        stacked = jnp.concatenate(
            [
                jnp.concatenate(
                    [spec_ref[d, 0, 0, c, at] for c in (0, 1) for d in range(devices)], axis=0
                )
                for at in (x, x + 1)
            ],
            axis=1,
        )
        done = on_rows(stacked, rows_ref)
        for at in (0, 1):
            piece = done[:, at * 2 * extent : (at + 1) * 2 * extent]
            re, im = piece[:half], piece[half:]
            reals.append(re * cosine - im * sine)
            imags.append(re * sine + im * cosine)
    real, imag = on_lanes(jnp.concatenate(reals, 0), jnp.concatenate(imags, 0), lanes_ref)
    first = pl.program_id(2) == 0
    for x in range(count):
        re, im = real[x * half : (x + 1) * half], imag[x * half : (x + 1) * half]
        part_real, part_imag = unpack(part_ref[0, x])
        top, bottom = pack(part_real * re - part_imag * im, part_real * im + part_imag * re)
        value = jnp.concatenate([top, bottom], axis=0)
        before = prior_ref[0, x] if chained else jnp.zeros_like(value)
        out_ref[0, x] = value + jnp.where(first, before, out_ref[0, x])


def turn(real, imag, step, count, sign):
    step = step % count
    if step == 0:
        return real, imag
    if 4 * step == count:
        return (-imag, real) if sign > 0 else (imag, -real)
    if 2 * step == count:
        return -real, -imag
    if 4 * step == 3 * count:
        return (imag, -real) if sign > 0 else (-imag, real)
    angle = 2.0 * math.pi * step / count
    cosine, sine = math.cos(angle), sign * math.sin(angle)
    return real * cosine - imag * sine, real * sine + imag * cosine


def small_dft(values, sign):
    count = len(values)
    if count == 1:
        return values
    even, odd = small_dft(values[0::2], sign), small_dft(values[1::2], sign)
    low, high = [], []
    for step in range(count // 2):
        turned_real, turned_imag = turn(*odd[step], step, count, sign)
        low.append((even[step][0] + turned_real, even[step][1] + turned_imag))
        high.append((even[step][0] - turned_real, even[step][1] - turned_imag))
    return low + high


def long_dft(values, sign):
    count, first = len(values), 1
    while first * first < count:
        first *= 2
    second = count // first
    columns = []
    for offset in range(second):
        part = small_dft(values[offset::second], sign)
        columns.append([turn(*part[k], offset * k, count, sign) for k in range(first)])
    out = [None] * count
    for k in range(first):
        for block, value in enumerate(small_dft([column[k] for column in columns], sign)):
            out[k + first * block] = value
    return out


def middle_kernel(first_ref, plane_ref, spec_ref, out_ref):
    field = pl.program_id(1)
    devices, slab = spec_ref.shape[0], spec_ref.shape[4]
    extent = devices * slab
    plane = plane_ref[0]
    values = [
        (spec_ref[x // slab, 0, 0, 0, x % slab], spec_ref[x // slab, 0, 0, 1, x % slab])
        for x in range(extent)
    ]
    values = long_dft(values, -1.0)
    scale = FOUR_PI / extent**3
    scaled = []
    for x, (real, imag) in enumerate(values):
        kernel = scale / (first_ref[field, x] + plane)
        scaled.append((real * kernel, imag * kernel))
    for x, (real, imag) in enumerate(long_dft(scaled, 1.0)):
        out_ref[x // slab, 0, 0, 0, x % slab] = real
        out_ref[x // slab, 0, 0, 1, x % slab] = imag


def whole_block(array):
    return pl.BlockSpec(array.shape, lambda *_: (0,) * array.ndim)


def chunk_of(slab):
    return math.gcd(slab, 8)


def cost(flops, count):
    return pl.CostEstimate(flops=int(flops), bytes_accessed=int(count), transcendentals=0)


def forward_call(orbitals, block, tables, devices):
    bands, slab, extent, lanes = orbitals.shape
    fields, step = block.shape[0], chunk_of(orbitals.shape[1])
    share = extent // 2 // devices
    grid_block = (1, step, extent, lanes)
    return pl.pallas_call(
        forward_kernel,
        grid=(bands, fields, slab // step),
        in_specs=[
            pl.BlockSpec(grid_block, lambda i, j, x: (i, x, 0, 0)),
            pl.BlockSpec(grid_block, lambda i, j, x: (j, x, 0, 0)),
        ]
        + [whole_block(table) for table in tables],
        out_specs=pl.BlockSpec(
            (devices, 1, 1, 2, step, share, lanes), lambda i, j, x: (0, i, j, 0, x, 0, 0)
        ),
        out_shape=jax.ShapeDtypeStruct(
            (devices, bands, fields, 2, slab, share, lanes), jnp.float32
        ),
        cost_estimate=cost(bands * fields * 1e9, bands * fields * orbitals[0].size * 12),
        name="forward",
    )(orbitals, block, *tables)


def middle_call(first_part, plane, spectrum):
    devices, bands, fields, _, slab, share, lanes = spectrum.shape
    spec = pl.BlockSpec(
        (devices, 1, 1, 2, slab, share, lanes), lambda i, j: (0, i, j, 0, 0, 0, 0)
    )
    return pl.pallas_call(
        middle_kernel,
        grid=(bands, fields),
        in_specs=[
            pl.BlockSpec(memory_space=pltpu.SMEM),
            pl.BlockSpec((1, share, lanes), lambda i, j: (j, 0, 0)),
            spec,
        ],
        out_specs=spec,
        out_shape=jax.ShapeDtypeStruct(spectrum.shape, jnp.float32),
        cost_estimate=cost(bands * fields * 1e9, spectrum.size * 8),
        name="middle",
    )(first_part, plane, spectrum)


def inverse_call(spectrum, block, prior, tables):
    devices, bands, fields, _, slab, share, lanes = spectrum.shape
    extent, step = block.shape[2], chunk_of(slab)
    grid_block = (1, step, extent, lanes)
    by_band = pl.BlockSpec(grid_block, lambda i, x, j: (i, x, 0, 0))
    chained = prior is not None
    extra = [prior] if chained else []
    body = lambda *refs: inverse_kernel(*refs, chained=chained)
    return pl.pallas_call(
        body,
        grid=(bands, slab // step, fields),
        in_specs=[
            pl.BlockSpec(
                (devices, 1, 1, 2, step, share, lanes), lambda i, x, j: (0, i, j, 0, x, 0, 0)
            ),
            pl.BlockSpec(grid_block, lambda i, x, j: (j, x, 0, 0)),
        ]
        + [by_band] * len(extra)
        + [whole_block(table) for table in tables],
        out_specs=by_band,
        out_shape=jax.ShapeDtypeStruct((bands, slab, extent, lanes), jnp.float32),
        cost_estimate=cost(bands * fields * 1e9, bands * fields * block[0].size * 12),
        name="inverse",
    )(spectrum, block, *extra, *tables)


def rotate(field):
    extent = field.shape[-1] // 2
    return jnp.concatenate([field[..., extent:], -field[..., :extent]], axis=-1)


def frequency(positions, extent):
    return jnp.where(positions < extent // 2, positions, positions - extent).astype(jnp.float32)


def kernel_parts(qvectors, row_start, row_count, extent):
    index = jnp.arange(extent, dtype=jnp.int32)
    parity = jnp.arange(2, dtype=jnp.int32)
    ky = 2 * (row_start + jnp.arange(row_count, dtype=jnp.int32))[:, None] + parity
    first = (frequency(index, extent)[None, :] + qvectors[:, 0:1]) ** 2
    second = (frequency(ky, extent)[None] + qvectors[:, 1, None, None]) ** 2
    third = (frequency(index, extent)[None, :] + qvectors[:, 2:3]) ** 2
    plane = second[:, :, :, None] + third[:, None, None, :] + SCREEN_SQUARE
    return first, plane.reshape(qvectors.shape[0], row_count, 2 * extent)


def factor_kernel(over_ref, inv_ref, *, order, scale):
    total = jnp.sum(over_ref[...], axis=0) * scale
    size = total.shape[-1]
    res_real, res_imag = total[0], total[1]
    rows = lax.broadcasted_iota(jnp.int32, (size, size), 0)
    cols = lax.broadcasted_iota(jnp.int32, (size, size), 1)
    same = rows == cols
    inv_real = jnp.where(same, 1.0, 0.0).astype(jnp.float32)
    inv_imag = jnp.zeros_like(inv_real)
    across = lambda v: jnp.sum(v, axis=1, keepdims=True)
    down = lambda v: jnp.sum(v, axis=0, keepdims=True)
    for step in range(order):
        at_col = cols == step
        pivot = down(across(jnp.where(at_col & (rows == step), res_real, 0.0)))
        root = 1.0 / jnp.sqrt(pivot)
        below = at_col & (rows > step)
        col_real = across(jnp.where(below, res_real, 0.0)) * root
        col_imag = across(jnp.where(below, res_imag, 0.0)) * root
        row_real = down(jnp.where(same, col_real, 0.0))
        row_imag = down(jnp.where(same, col_imag, 0.0))
        res_real = res_real - (col_real * row_real + col_imag * row_imag)
        res_imag = res_imag - (col_imag * row_real - col_real * row_imag)
        at_row = rows == step
        inv_real = jnp.where(at_row, inv_real * root, inv_real)
        inv_imag = jnp.where(at_row, inv_imag * root, inv_imag)
        lead_real = down(jnp.where(at_row, inv_real, 0.0))
        lead_imag = down(jnp.where(at_row, inv_imag, 0.0))
        inv_real = inv_real - (col_real * lead_real - col_imag * lead_imag)
        inv_imag = inv_imag - (col_real * lead_imag + col_imag * lead_real)
    inv_ref[0] = inv_real
    inv_ref[1] = inv_imag


def factor_inverse(pieces, order, scale):
    size = pieces.shape[-1]
    body = lambda a, b: factor_kernel(a, b, order=order, scale=scale)
    return pl.pallas_call(
        body, out_shape=jax.ShapeDtypeStruct((2, size, size), jnp.float32), name="factor"
    )(pieces)


def ring_shift(value, axis_name, count, step):
    return lax.ppermute(value, axis_name, [(i, (i + step) % count) for i in range(count)])


def gather_small(value, axis_name, count):
    copies = jnp.broadcast_to(value[None], (count,) + value.shape)
    return lax.all_to_all(copies, axis_name, split_axis=0, concat_axis=0, tiled=True)


def groups_of(count):
    if count < 4:
        return [[step] for step in range(count)]
    middle = list(range(1, count))
    middle.remove(count // 2)
    return [[0], middle, [count // 2]]


def exchange_body(band_size, fft_size, orbitals, partners, shift_table, shift_index):
    extent = orbitals.shape[2]
    band_count, slab = orbitals.shape[:2]
    partner_count = partners.shape[0]
    row_count = extent // 2 // fft_size
    my_band = lax.axis_index("band")
    row_start = lax.axis_index("fft") * row_count
    forward_tables = stage_tables(extent, -1.0)
    inverse_tables = stage_tables(extent, 1.0)

    arrived = [partners] + [
        ring_shift(partners, "band", band_size, step) for step in range(1, band_size)
    ]
    potential = None
    for steps in groups_of(band_size):
        block = jnp.concatenate([arrived[step] for step in steps], axis=0)
        ids = jnp.concatenate(
            [
                (my_band - step) % band_size * partner_count + jnp.arange(partner_count)
                for step in steps
            ]
        )
        first, plane = kernel_parts(
            shift_table[shift_index[ids]], row_start, row_count, extent
        )
        spectrum = forward_call(orbitals, block, forward_tables, fft_size)
        spectrum = lax.all_to_all(spectrum, "fft", split_axis=0, concat_axis=0, tiled=True)
        spectrum = middle_call(first, plane, spectrum)
        spectrum = lax.all_to_all(spectrum, "fft", split_axis=0, concat_axis=0, tiled=True)
        potential = inverse_call(spectrum, block, potential, inverse_tables)

    def spread(value):
        rows = value.reshape(band_count, band_size, -1, 2 * extent).swapaxes(0, 1)
        rows = lax.all_to_all(rows, "band", split_axis=0, concat_axis=0, tiled=True)
        return rows.reshape(band_count * band_size, -1, 2 * extent)

    sub_orbitals = spread(orbitals)
    sub_pot = spread(potential)
    total_bands = sub_pot.shape[0]
    sub_turned = rotate(sub_pot)
    flat_pot = sub_pot.reshape(total_bands, -1)
    flat_turned = sub_turned.reshape(total_bands, -1)
    both = jnp.stack([flat_pot, flat_turned])
    over = jnp.einsum("ik,cjk->cij", sub_orbitals.reshape(total_bands, -1), both, precision=PREC)
    size = max(8, total_bands)
    over = jnp.pad(over, ((0, 0), (0, size - total_bands), (0, size - total_bands)))
    pieces = gather_small(over, ("band", "fft"), band_size * fft_size)
    inverse = factor_inverse(pieces, total_bands, 1.0 / float(extent**3))
    inverse = inverse[:, :total_bands, :total_bands]
    projector = jnp.einsum("clm,cmk->lk", inverse, both, precision=PREC)
    projector = projector.reshape(band_size, band_count, -1, 2 * extent)
    projector = lax.all_to_all(projector, "band", split_axis=0, concat_axis=0, tiled=True)
    return (potential, projector.swapaxes(0, 1).reshape(orbitals.shape))


def solution(mesh):
    spec = P(("kgrp", "band"), "fft", None, None)
    band_size, fft_size = mesh.shape["band"], mesh.shape["fft"]
    body = lambda *arrays: exchange_body(band_size, fft_size, *arrays)
    return jax.shard_map(
        body,
        mesh=mesh,
        in_specs=(spec, spec, P(), P("kgrp")),
        out_specs=(spec, spec),
        check_vma=False,
    )
```

profile of v0, /device:TPU:0, one launch (start us, length us, event | category | flops | bytes accessed | tf_op | source)
XLA Modules:
  0.0 190.5 jit_solution(16029930305961354760)
XLA Ops:
  0.6 3.1 %collective-permute-start.1 = (f32[1,16,64,128]{3,2,1,0:T(8,128)}, f32[1,16,64,128]{3,2,1,0:T(8,128)S(1)}, u32[]{:S(2)}, u32[]{:S(2)}) collective-permute-start(f32[1,16,64,128]{3,2,1,0:T(8,128)} %refs_1_.1), channel_id=1, source_target_pairs={{0,4},{4,8},{8,12},{12,0},{1,5},{5,9},{9,13},{13,1},{2,6},{6,10},{... | collective-permute-start | bytes 1572872 | tf_op jit(solution)/shard_map/ppermute | solution.py:363
  3.7 2.1 %collective-permute-start.2 = (f32[1,16,64,128]{3,2,1,0:T(8,128)}, f32[1,16,64,128]{3,2,1,0:T(8,128)S(1)}, u32[]{:S(2)}, u32[]{:S(2)}) collective-permute-start(f32[1,16,64,128]{3,2,1,0:T(8,128)} %refs_1_.1), channel_id=1, source_target_pairs={{0,12},{4,0},{8,4},{12,8},{1,13},{5,1},{9,5},{13,9},{2,14},{6,2},{... | collective-permute-start | bytes 1572872 | tf_op jit(solution)/shard_map/ppermute | solution.py:363
  6.8 3.1 %forward.5 = f32[4,1,1,2,16,8,128]{6,5,4,3,2,1,0:T(8,128)} custom-call(f32[1,16,64,128]{3,2,1,0:T(8,128)} %orb_ref.5, f32[1,16,64,128]{3,2,1,0:T(8,128)} %refs_1_.1, bf16[2,256,256]{2,1,0:T(8,128)(2,1)} %constant.172.lanes_ref, bf16[64,192]{1,0:T(8,128)(2,1)} %constant.86.clone.rows_ref, f32[2,32,128]{2,1,0:T(8,128)} %constant.87.clone.twid_ref), custom_call_target="tpu_custom_call" | custom-call | flops 1000000000 | bytes 1572864 | tf_op jit(solution)/shard_map/forward/pallas_call | solution.py:236
  9.9 3.5 %all-to-all-start.4 = ((f32[4,1,1,2,16,8,128]{6,5,4,3,2,1,0:T(8,128)}), f32[4,1,1,2,16,8,128]{6,5,4,3,2,1,0:T(8,128)S(1)}, u32[]{:S(2)}, u32[]{:S(2)}) async-start(f32[4,1,1,2,16,8,128]{6,5,4,3,2,1,0:T(8,128)} %forward.5), calls=%async_computation.4 | async-start | bytes 1048576 | tf_op jit(solution)/shard_map/all_to_all | solution.py:405
  20.7 1.3 add_multiply_fusion.1
  26.2 2.3 %middle.5 = f32[4,1,1,2,16,8,128]{6,5,4,3,2,1,0:T(8,128)} custom-call(f32[1,64]{1,0:T(1,128)} %add_multiply_fusion.6.first_ref, f32[1,8,128]{2,1,0:T(8,128)} %add_add_fusion.1.plane_ref, f32[4,1,1,2,16,8,128]{6,5,4,3,2,1,0:T(8,128)} %copy-done.2), custom_call_target="tpu_custom_call" | custom-call | flops 1000000000 | bytes 1048576 | tf_op jit(solution)/shard_map/middle/pallas_call | solution.py:260
  28.6 3.5 %all-to-all-start.5 = ((f32[4,1,1,2,16,8,128]{6,5,4,3,2,1,0:T(8,128)}), f32[4,1,1,2,16,8,128]{6,5,4,3,2,1,0:T(8,128)S(1)}, u32[]{:S(2)}, u32[]{:S(2)}) async-start(f32[4,1,1,2,16,8,128]{6,5,4,3,2,1,0:T(8,128)} %middle.5), calls=%async_computation.5 | async-start | bytes 1048576 | tf_op jit(solution)/shard_map/all_to_all | solution.py:407
  32.1 19.5 %collective-permute-done.part_ref.refs_1_ = f32[1,16,64,128]{3,2,1,0:T(8,128)S(1)} collective-permute-done((f32[1,16,64,128]{3,2,1,0:T(8,128)}, f32[1,16,64,128]{3,2,1,0:T(8,128)S(1)}, u32[]{:S(2)}, u32[]{:S(2)}) %collective-permute-start) | collective-permute-done | bytes 524320 | tf_op jit(solution)/shard_map/ppermute | solution.py:363
  52.4 3.1 %forward.3 = f32[4,1,1,2,16,8,128]{6,5,4,3,2,1,0:T(8,128)} custom-call(f32[1,16,64,128]{3,2,1,0:T(8,128)} %orb_ref.5, f32[1,16,64,128]{3,2,1,0:T(8,128)} %copy-done.8, bf16[2,256,256]{2,1,0:T(8,128)(2,1)} %constant.172.lanes_ref, bf16[64,192]{1,0:T(8,128)(2,1)} %constant.86.clone.rows_ref, f32[2,32,128]{2,1,0:T(8,128)} %constant.87.clone.twid_ref), custom_call_target="tpu_custom_call" | custom-call | flops 1000000000 | bytes 1572864 | tf_op jit(solution)/shard_map/forward/pallas_call | solution.py:236
  56.3 3.5 %all-to-all-start = ((f32[4,1,1,2,16,8,128]{6,5,4,3,2,1,0:T(8,128)}), f32[4,1,1,2,16,8,128]{6,5,4,3,2,1,0:T(8,128)S(1)}, u32[]{:S(2)}, u32[]{:S(2)}) async-start(f32[4,1,1,2,16,8,128]{6,5,4,3,2,1,0:T(8,128)} %forward.3), calls=%async_computation | async-start | bytes 1048576 | tf_op jit(solution)/shard_map/all_to_all | solution.py:405
  60.9 4.9 %forward.4 = f32[4,1,2,2,16,8,128]{6,5,4,3,2,1,0:T(8,128)} custom-call(f32[1,16,64,128]{3,2,1,0:T(8,128)} %orb_ref.5, f32[2,16,64,128]{3,2,1,0:T(8,128)} %copy-done.6, bf16[2,256,256]{2,1,0:T(8,128)(2,1)} %constant.172.lanes_ref, bf16[64,192]{1,0:T(8,128)(2,1)} %constant.86.clone.rows_ref, f32[2,32,128]{2,1,0:T(8,128)} %constant.87.clone.twid_ref), custom_call_target="tpu_custom_call" | custom-call | flops 2000000000 | bytes 3145728 | tf_op jit(solution)/shard_map/forward/pallas_call | solution.py:236
  65.9 2.7 %all-to-all-done.spec_ref = f32[4,1,1,2,16,8,128]{6,5,4,3,2,1,0:T(8,128)S(1)} async-done(((f32[4,1,1,2,16,8,128]{6,5,4,3,2,1,0:T(8,128)}), f32[4,1,1,2,16,8,128]{6,5,4,3,2,1,0:T(8,128)S(1)}, u32[]{:S(2)}, u32[]{:S(2)}) %all-to-all-start) | async-done | bytes 524320 | tf_op jit(solution)/shard_map/all_to_all | solution.py:405
  69.4 3.5 %all-to-all-start.2 = ((f32[4,1,2,2,16,8,128]{6,5,4,3,2,1,0:T(8,128)}), f32[4,1,2,2,16,8,128]{6,5,4,3,2,1,0:T(8,128)S(1)}, u32[]{:S(2)}, u32[]{:S(2)}) async-start(f32[4,1,2,2,16,8,128]{6,5,4,3,2,1,0:T(8,128)} %forward.4), calls=%async_computation.2 | async-start | bytes 2097152 | tf_op jit(solution)/shard_map/all_to_all | solution.py:405
  74.8 1.2 add_multiply_fusion.9.first_ref
  76.6 2.3 %middle.3 = f32[4,1,1,2,16,8,128]{6,5,4,3,2,1,0:T(8,128)} custom-call(f32[1,64]{1,0:T(1,128)} %add_multiply_fusion.9.first_ref, f32[1,8,128]{2,1,0:T(8,128)} %add_add_fusion.2.plane_ref, f32[4,1,1,2,16,8,128]{6,5,4,3,2,1,0:T(8,128)} %copy-done.4), custom_call_target="tpu_custom_call" | custom-call | flops 1000000000 | bytes 1048576 | tf_op jit(solution)/shard_map/middle/pallas_call | solution.py:260
  78.9 8.4 %all-to-all-done.2.spec_ref = f32[4,1,2,2,16,8,128]{6,5,4,3,2,1,0:T(8,128)S(1)} async-done(((f32[4,1,2,2,16,8,128]{6,5,4,3,2,1,0:T(8,128)}), f32[4,1,2,2,16,8,128]{6,5,4,3,2,1,0:T(8,128)S(1)}, u32[]{:S(2)}, u32[]{:S(2)}) %all-to-all-start.2) | async-done | bytes 1048608 | tf_op jit(solution)/shard_map/all_to_all | solution.py:405
  87.3 3.5 %all-to-all-start.1 = ((f32[4,1,1,2,16,8,128]{6,5,4,3,2,1,0:T(8,128)}), f32[4,1,1,2,16,8,128]{6,5,4,3,2,1,0:T(8,128)S(1)}, u32[]{:S(2)}, u32[]{:S(2)}) async-start(f32[4,1,1,2,16,8,128]{6,5,4,3,2,1,0:T(8,128)} %middle.3), calls=%async_computation.1 | async-start | bytes 1048576 | tf_op jit(solution)/shard_map/all_to_all | solution.py:407
  91.4 2.8 %middle.4 = f32[4,1,2,2,16,8,128]{6,5,4,3,2,1,0:T(8,128)} custom-call(f32[2,64]{1,0:T(2,128)} %get-tuple-element.64.first_ref, f32[2,8,128]{2,1,0:T(8,128)} %add_add_fusion.plane_ref, f32[4,1,2,2,16,8,128]{6,5,4,3,2,1,0:T(8,128)} %copy-done.1), custom_call_target="tpu_custom_call" | custom-call | flops 2000000000 | bytes 2097152 | tf_op jit(solution)/shard_map/middle/pallas_call | solution.py:260
  94.2 5.4 %all-to-all-done.1.refs_0_ = f32[4,1,1,2,16,8,128]{6,5,4,3,2,1,0:T(8,128)S(1)} async-done(((f32[4,1,1,2,16,8,128]{6,5,4,3,2,1,0:T(8,128)}), f32[4,1,1,2,16,8,128]{6,5,4,3,2,1,0:T(8,128)S(1)}, u32[]{:S(2)}, u32[]{:S(2)}) %all-to-all-start.1) | async-done | bytes 524320 | tf_op jit(solution)/shard_map/all_to_all | solution.py:407
  99.6 18.7 %all_to_all.50.refs_0_ = f32[4,1,2,2,16,8,128]{6,5,4,3,2,1,0:T(8,128)} all-to-all(f32[4,1,2,2,16,8,128]{6,5,4,3,2,1,0:T(8,128)} %middle.4), channel_id=1, replica_groups=mesh['kgrp'=2,'band'=4,'fft'=4] {'fft'}, dimensions={0} | all-to-all | bytes 2097152 | tf_op jit(solution)/shard_map/all_to_all | solution.py:407
  118.3 3.5 %all-to-all-start.7 = ((f32[4,1,256,128]{3,2,1,0:T(8,128)}), f32[4,1,256,128]{3,2,1,0:T(8,128)S(1)}, u32[]{:S(2)}, u32[]{:S(2)}) async-start(f32[4,1,256,128]{3,2,1,0:T(8,128)} %bitcast.20), calls=%async_computation.7 | async-start | bytes 1048576 | tf_op jit(solution)/shard_map/all_to_all | solution.py:412
  121.8 2.9 %inverse.3.refs_2_ = f32[1,16,64,128]{3,2,1,0:T(8,128)} custom-call(f32[4,1,1,2,16,8,128]{6,5,4,3,2,1,0:T(8,128)} %copy-done.3, f32[1,16,64,128]{3,2,1,0:T(8,128)} %refs_1_.1, bf16[2,256,256]{2,1,0:T(8,128)(2,1)} %constant.175.refs_2_.refs_3_, bf16[64,192]{1,0:T(8,128)(2,1)} %constant.90.clone.refs_3_.refs_4_, f32[2,32,128]{2,1,0:T(8,128)} %constant.91.clone.refs_4_.refs_5_), custom_call_target="tpu_custom_call" | custom-call | flops 1000000000 | bytes 1572864 | tf_op jit(solution)/shard_map/inverse/pallas_call | solution.py:283
  124.7 4.6 %inverse.4.refs_2_ = f32[1,16,64,128]{3,2,1,0:T(8,128)} custom-call(f32[4,1,2,2,16,8,128]{6,5,4,3,2,1,0:T(8,128)} %all_to_all.50.refs_0_, f32[2,16,64,128]{3,2,1,0:T(8,128)} %copy-done.6, f32[1,16,64,128]{3,2,1,0:T(8,128)} %inverse.3.refs_2_, bf16[2,256,256]{2,1,0:T(8,128)(2,1)} %constant.175.refs_2_.refs_3_, ...), custom_call_target="tpu_custom_call" | custom-call | flops 2000000000 | bytes 3145728 | tf_op jit(solution)/shard_map/inverse/pallas_call | solution.py:283
  129.3 2.9 %inverse.5 = f32[1,16,64,128]{3,2,1,0:T(8,128)} custom-call(f32[4,1,1,2,16,8,128]{6,5,4,3,2,1,0:T(8,128)} %copy-done.5, f32[1,16,64,128]{3,2,1,0:T(8,128)} %copy-done.8, f32[1,16,64,128]{3,2,1,0:T(8,128)} %inverse.4.refs_2_, bf16[2,256,256]{2,1,0:T(8,128)(2,1)} %constant.175.refs_2_.refs_3_, bf16[64,192]{1,0:T(8,128)(2,1)} %constant.90.clone.refs_3_.refs_4_, ...), custom_call_target="tpu_custom_call" | custom-call | flops 1000000000 | bytes 1572864 | tf_op jit(solution)/shard_map/inverse/pallas_call | solution.py:283
  132.2 3.9 %all-to-all-done.7 = f32[4,1,256,128]{3,2,1,0:T(8,128)S(1)} async-done(((f32[4,1,256,128]{3,2,1,0:T(8,128)}), f32[4,1,256,128]{3,2,1,0:T(8,128)S(1)}, u32[]{:S(2)}, u32[]{:S(2)}) %all-to-all-start.7) | async-done | bytes 524320 | tf_op jit(solution)/shard_map/all_to_all | solution.py:412
  136.2 3.5 %all-to-all-start.6 = ((f32[4,1,256,128]{3,2,1,0:T(8,128)}), f32[4,1,256,128]{3,2,1,0:T(8,128)S(1)}, u32[]{:S(2)}, u32[]{:S(2)}) async-start(f32[4,1,256,128]{3,2,1,0:T(8,128)} %bitcast.49), calls=%async_computation.6 | async-start | bytes 1048576 | tf_op jit(solution)/shard_map/all_to_all | solution.py:412
  139.9 13.8 %all-to-all-done.6 = f32[4,1,256,128]{3,2,1,0:T(8,128)S(1)} async-done(((f32[4,1,256,128]{3,2,1,0:T(8,128)}), f32[4,1,256,128]{3,2,1,0:T(8,128)S(1)}, u32[]{:S(2)}, u32[]{:S(2)}) %all-to-all-start.6) | async-done | bytes 524320 | tf_op jit(solution)/shard_map/all_to_all | solution.py:412
  154.6 2.9 %convolution_bitcast_fusion.1 = f32[2,4,4]{1,2,0:T(4,128)S(1)} fusion(f32[2,4,32768]{2,1,0:T(4,128)S(1)} %constant_dynamic-update-slice_fusion.2, f32[4,32768,1]{1,0,2:T(4,128)S(1)} %reshape.487), kind=kOutput, calls=%fused_computation.3 | convolution fusion | flops 6291456 | bytes 1572992 | tf_op jit(solution)/shard_map/ik,cjk->cij/dot_general | solution.py:422
  157.8 9.3 %all_to_all.51 = f32[16,1,128]{2,1,0:T(1,128)S(1)} all-to-all(f32[16,1,128]{2,1,0:T(1,128)S(1)} %reshape.493), channel_id=1, replica_groups=mesh['kgrp'=2,'band'=4,'fft'=4] {'band','fft'}, dimensions={0} | all-to-all | bytes 16384 | tf_op jit(solution)/shard_map/all_to_all | solution.py:368
  169.1 1.9 %factor.1 = f32[2,8,8]{2,1,0:T(8,128)} custom-call(f32[16,2,8,8]{3,2,1,0:T(8,128)} %reshape.494.a), custom_call_target="tpu_custom_call" | custom-call | tf_op jit(solution)/shard_map/factor/pallas_call | solution.py:357
  171.0 1.5 convolution_bitcast_fusion
  172.6 17.1 %all_to_all.52 = f32[4,1,256,128]{3,2,1,0:T(8,128)S(1)} all-to-all(f32[4,1,256,128]{3,2,1,0:T(8,128)S(1)} %bitcast.47), channel_id=1, replica_groups=mesh['kgrp'=2,'band'=4,'fft'=4] {'band'}, dimensions={0} | all-to-all | bytes 1048576 | tf_op jit(solution)/shard_map/all_to_all | solution.py:430
  (75 shorter events, 19.3 us)
Async XLA Ops:
  0.6 59.2 %collective-permute-start.1 = (f32[1,16,64,128]{3,2,1,0:T(8,128)}, f32[1,16,64,128]{3,2,1,0:T(8,128)S(1)}, u32[]{:S(2)}, u32[]{:S(2)}) collective-permute-start(f32[1,16,64,128]{3,2,1,0:T(8,128)} %refs_1_.1), channel_id=1, source_target_pairs={{0,4},{4,8},{8,12},{12,0},{1,5},{5,9},{9,13},{13,1},{2,6},{6,10},{... | collective-permute-start | bytes 1572872 | tf_op jit(solution)/shard_map/ppermute | solution.py:363
  3.7 56.1 %collective-permute-start.2 = (f32[1,16,64,128]{3,2,1,0:T(8,128)}, f32[1,16,64,128]{3,2,1,0:T(8,128)S(1)}, u32[]{:S(2)}, u32[]{:S(2)}) collective-permute-start(f32[1,16,64,128]{3,2,1,0:T(8,128)} %refs_1_.1), channel_id=1, source_target_pairs={{0,12},{4,0},{8,4},{12,8},{1,13},{5,1},{9,5},{13,9},{2,14},{6,2},{... | collective-permute-start | bytes 1572872 | tf_op jit(solution)/shard_map/ppermute | solution.py:363
  5.8 45.8 %collective-permute-start = (f32[1,16,64,128]{3,2,1,0:T(8,128)}, f32[1,16,64,128]{3,2,1,0:T(8,128)S(1)}, u32[]{:S(2)}, u32[]{:S(2)}) collective-permute-start(f32[1,16,64,128]{3,2,1,0:T(8,128)} %refs_1_.1), channel_id=1, source_target_pairs={{0,8},{4,12},{8,0},{12,4},{1,9},{5,13},{9,1},{13,5},{2,10},{6,14},... | collective-permute-start | bytes 1572872 | tf_op jit(solution)/shard_map/ppermute | solution.py:363
  9.9 15.5 %all-to-all-start.4 = ((f32[4,1,1,2,16,8,128]{6,5,4,3,2,1,0:T(8,128)}), f32[4,1,1,2,16,8,128]{6,5,4,3,2,1,0:T(8,128)S(1)}, u32[]{:S(2)}, u32[]{:S(2)}) async-start(f32[4,1,1,2,16,8,128]{6,5,4,3,2,1,0:T(8,128)} %forward.5), calls=%async_computation.4 | async-start | bytes 1048576 | tf_op jit(solution)/shard_map/all_to_all | solution.py:405
  13.5 0.7 copy-start
  18.0 0.7 copy-start.7
  25.5 0.8 copy-start.2
  28.6 27.0 %all-to-all-start.5 = ((f32[4,1,1,2,16,8,128]{6,5,4,3,2,1,0:T(8,128)}), f32[4,1,1,2,16,8,128]{6,5,4,3,2,1,0:T(8,128)S(1)}, u32[]{:S(2)}, u32[]{:S(2)}) async-start(f32[4,1,1,2,16,8,128]{6,5,4,3,2,1,0:T(8,128)} %middle.5), calls=%async_computation.5 | async-start | bytes 1048576 | tf_op jit(solution)/shard_map/all_to_all | solution.py:407
  51.6 0.8 copy-start.8
  55.5 0.8 copy-start.3
  56.3 12.3 %all-to-all-start = ((f32[4,1,1,2,16,8,128]{6,5,4,3,2,1,0:T(8,128)}), f32[4,1,1,2,16,8,128]{6,5,4,3,2,1,0:T(8,128)S(1)}, u32[]{:S(2)}, u32[]{:S(2)}) async-start(f32[4,1,1,2,16,8,128]{6,5,4,3,2,1,0:T(8,128)} %forward.3), calls=%async_computation | async-start | bytes 1048576 | tf_op jit(solution)/shard_map/all_to_all | solution.py:405
  59.9 1.0 copy-start.6
  68.6 0.8 copy-start.4
  69.4 17.9 %all-to-all-start.2 = ((f32[4,1,2,2,16,8,128]{6,5,4,3,2,1,0:T(8,128)}), f32[4,1,2,2,16,8,128]{6,5,4,3,2,1,0:T(8,128)S(1)}, u32[]{:S(2)}, u32[]{:S(2)}) async-start(f32[4,1,2,2,16,8,128]{6,5,4,3,2,1,0:T(8,128)} %forward.4), calls=%async_computation.2 | async-start | bytes 2097152 | tf_op jit(solution)/shard_map/all_to_all | solution.py:405
  87.3 4.1 %copy-start.1 = (f32[4,1,2,2,16,8,128]{6,5,4,3,2,1,0:T(8,128)}, f32[4,1,2,2,16,8,128]{6,5,4,3,2,1,0:T(8,128)S(1)}, u32[]{:S(2)}) copy-start(f32[4,1,2,2,16,8,128]{6,5,4,3,2,1,0:T(8,128)S(1)} %all-to-all-done.2.spec_ref) | copy-start | bytes 3145732
  87.3 12.3 %all-to-all-start.1 = ((f32[4,1,1,2,16,8,128]{6,5,4,3,2,1,0:T(8,128)}), f32[4,1,1,2,16,8,128]{6,5,4,3,2,1,0:T(8,128)S(1)}, u32[]{:S(2)}, u32[]{:S(2)}) async-start(f32[4,1,1,2,16,8,128]{6,5,4,3,2,1,0:T(8,128)} %middle.3), calls=%async_computation.1 | async-start | bytes 1048576 | tf_op jit(solution)/shard_map/all_to_all | solution.py:407
  99.6 18.7 %copy-start.5 = (f32[4,1,1,2,16,8,128]{6,5,4,3,2,1,0:T(8,128)}, f32[4,1,1,2,16,8,128]{6,5,4,3,2,1,0:T(8,128)S(1)}, u32[]{:S(2)}) copy-start(f32[4,1,1,2,16,8,128]{6,5,4,3,2,1,0:T(8,128)S(1)} %all-to-all-done.1.refs_0_) | copy-start | bytes 1572868
  118.3 17.9 %all-to-all-start.7 = ((f32[4,1,256,128]{3,2,1,0:T(8,128)}), f32[4,1,256,128]{3,2,1,0:T(8,128)S(1)}, u32[]{:S(2)}, u32[]{:S(2)}) async-start(f32[4,1,256,128]{3,2,1,0:T(8,128)} %bitcast.20), calls=%async_computation.7 | async-start | bytes 1048576 | tf_op jit(solution)/shard_map/all_to_all | solution.py:412
  136.2 17.5 %all-to-all-start.6 = ((f32[4,1,256,128]{3,2,1,0:T(8,128)}), f32[4,1,256,128]{3,2,1,0:T(8,128)S(1)}, u32[]{:S(2)}, u32[]{:S(2)}) async-start(f32[4,1,256,128]{3,2,1,0:T(8,128)} %bitcast.49), calls=%async_computation.6 | async-start | bytes 1048576 | tf_op jit(solution)/shard_map/all_to_all | solution.py:412
where the time goes:
time: 192 us; the launch traced here: 190 us
  waiting for transfers between devices  53.7 us (28%)
  blocking collectives  45.2 us (24%)
  Pallas kernels  31.1 us (16%)
  starting transfers between devices  30.5 us (16%)
  local copies, waits for them, and re-layouts  12.2 us (6%)
  other arithmetic  8.73 us (5%)
  between operations  4.74 us (2%)
  matrix products  4.4 us (2%)
    ppermute x3, waiting for transfers between devices, ring_shift(): lax.ppermute(value, axis_name, [(i, (i + step) % count) for i in range(co...  19.5 us
    all_to_all x1, blocking collectives, exchange_body(): lax.all_to_all(spectrum, 'fft', split_axis=0, concat_axis=0, tiled=True)  18.7 us
    all_to_all x2, waiting for transfers between devices, spread(): rows = lax.all_to_all(rows, 'band', split_axis=0, concat_axis=0, tiled=True)  17.7 us
    all_to_all x5, starting transfers between devices, exchange_body(): lax.all_to_all(spectrum, 'fft', split_axis=0, concat_axis=0, tiled=True)  17.4 us
    all_to_all x1, blocking collectives, exchange_body(): lax.all_to_all(projector, 'band', split_axis=0, concat_axis=0, tiled=True)  17.1 us
    all_to_all x5, waiting for transfers between devices, exchange_body(): lax.all_to_all(spectrum, 'fft', split_axis=0, concat_axis=0, tiled=True)  16.5 us
    pallas_call x3, Pallas kernels, forward_call(): pl.pallas_call(forward_kernel, grid=(bands, fields, slab // step), in_spe...  11.2 us
    pallas_call x3, Pallas kernels, inverse_call(): pl.pallas_call(body, grid=(bands, slab // step, fields), in_specs=[pl.Blo...  10.4 us
  transfers between devices with their start and end apart: 10, of which 6 were waited for; matrix products, arithmetic and copies ran while one was open for 6% of the time, Pallas kernels for 15%

commit v1 on v0

--- a/solution.py
+++ b/solution.py
@@ -7,6 +7,7 @@
 from jax.experimental import pallas as pl
 from jax.experimental.pallas import tpu as pltpu
 from jax.sharding import PartitionSpec as P
+
 
 PREC = lax.Precision.HIGH
 SCREEN_SQUARE = 0.25
@@ -196,8 +197,8 @@
     return out
 
 
-def middle_kernel(first_ref, plane_ref, spec_ref, out_ref):
-    field = pl.program_id(1)
+def middle_kernel(first_ref, plane_ref, spec_ref, out_ref, *, start):
+    field = pl.program_id(1) + start
     devices, slab = spec_ref.shape[0], spec_ref.shape[4]
     extent = devices * slab
     plane = plane_ref[0]
@@ -252,17 +253,18 @@
     )(orbitals, block, *tables)
 
 
-def middle_call(first_part, plane, spectrum):
+def middle_call(first_part, plane, start, spectrum):
     devices, bands, fields, _, slab, share, lanes = spectrum.shape
     spec = pl.BlockSpec(
         (devices, 1, 1, 2, slab, share, lanes), lambda i, j: (0, i, j, 0, 0, 0, 0)
     )
+    body = lambda *refs: middle_kernel(*refs, start=start)
     return pl.pallas_call(
-        middle_kernel,
+        body,
         grid=(bands, fields),
         in_specs=[
             pl.BlockSpec(memory_space=pltpu.SMEM),
-            pl.BlockSpec((1, share, lanes), lambda i, j: (j, 0, 0)),
+            pl.BlockSpec((1, share, lanes), lambda i, j: (j + start, 0, 0)),
             spec,
         ],
         out_specs=spec,
@@ -359,26 +361,27 @@
     )(pieces)
 
 
-def ring_shift(value, axis_name, count, step):
-    return lax.ppermute(value, axis_name, [(i, (i + step) % count) for i in range(count)])
-
-
 def gather_small(value, axis_name, count):
     copies = jnp.broadcast_to(value[None], (count,) + value.shape)
     return lax.all_to_all(copies, axis_name, split_axis=0, concat_axis=0, tiled=True)
 
 
-def groups_of(count):
-    if count < 4:
-        return [[step] for step in range(count)]
-    middle = list(range(1, count))
-    middle.remove(count // 2)
-    return [[0], middle, [count // 2]]
+def source_of(place, step, count):
+    return place ^ step if count & (count - 1) == 0 else (place - step) % count
+
+
+def fetch(value, step, count):
+    pairs = [(source_of(place, step, count), place) for place in range(count)]
+    return lax.ppermute(value, "band", pairs)
+
+
+def after(value, earlier):
+    return lax.optimization_barrier((value, earlier))[0]
 
 
 def exchange_body(band_size, fft_size, orbitals, partners, shift_table, shift_index):
     extent = orbitals.shape[2]
-    band_count, slab = orbitals.shape[:2]
+    band_count, _ = orbitals.shape[:2]
     partner_count = partners.shape[0]
     row_count = extent // 2 // fft_size
     my_band = lax.axis_index("band")
@@ -386,33 +389,47 @@
     forward_tables = stage_tables(extent, -1.0)
     inverse_tables = stage_tables(extent, 1.0)
 
-    arrived = [partners] + [
-        ring_shift(partners, "band", band_size, step) for step in range(1, band_size)
-    ]
-    potential = None
-    for steps in groups_of(band_size):
-        block = jnp.concatenate([arrived[step] for step in steps], axis=0)
-        ids = jnp.concatenate(
-            [
-                (my_band - step) % band_size * partner_count + jnp.arange(partner_count)
-                for step in steps
-            ]
-        )
-        first, plane = kernel_parts(
-            shift_table[shift_index[ids]], row_start, row_count, extent
-        )
-        spectrum = forward_call(orbitals, block, forward_tables, fft_size)
-        spectrum = lax.all_to_all(spectrum, "fft", split_axis=0, concat_axis=0, tiled=True)
-        spectrum = middle_call(first, plane, spectrum)
-        spectrum = lax.all_to_all(spectrum, "fft", split_axis=0, concat_axis=0, tiled=True)
-        potential = inverse_call(spectrum, block, potential, inverse_tables)
-
     def spread(value):
         rows = value.reshape(band_count, band_size, -1, 2 * extent).swapaxes(0, 1)
         rows = lax.all_to_all(rows, "band", split_axis=0, concat_axis=0, tiled=True)
         return rows.reshape(band_count * band_size, -1, 2 * extent)
 
-    sub_orbitals = spread(orbitals)
+    arrived, ids = [partners], []
+    for step in range(1, band_size):
+        source = after(partners, arrived[-1]) if step > 2 else partners
+        arrived.append(fetch(source, step, band_size))
+    for step in range(band_size):
+        owner = source_of(my_band, step, band_size)
+        ids.append(owner * partner_count + jnp.arange(partner_count))
+    qvectors = shift_table[shift_index[jnp.concatenate(ids)]]
+    first, plane = kernel_parts(qvectors, row_start, row_count, extent)
+
+    spectra, middles, potential, done = [], [], None, 0
+
+    def finish(potential):
+        return inverse_call(spectra[done], arrived[done], potential, inverse_tables)
+
+    for step in range(band_size):
+        block = arrived[step]
+        if step >= 1:
+            block = after(block, middles[-1])
+        if step >= 2:
+            potential = finish(potential)
+            done += 1
+            block = after(block, potential)
+        sent = forward_call(orbitals, block, forward_tables, fft_size)
+        spectrum = lax.all_to_all(sent, "fft", split_axis=0, concat_axis=0, tiled=True)
+        spectrum = middle_call(first, plane, step * partner_count, spectrum)
+        middles.append(spectrum)
+        if step == band_size - 1:
+            sub_orbitals = spread(after(orbitals, sent))
+            spectrum = after(spectrum, sub_orbitals)
+        spectrum = lax.all_to_all(spectrum, "fft", split_axis=0, concat_axis=0, tiled=True)
+        spectra.append(spectrum)
+    while done < band_size:
+        potential = finish(potential)
+        done += 1
+
     sub_pot = spread(potential)
     total_bands = sub_pot.shape[0]
     sub_turned = rotate(sub_pot)
@@ -434,7 +451,10 @@
 def solution(mesh):
     spec = P(("kgrp", "band"), "fft", None, None)
     band_size, fft_size = mesh.shape["band"], mesh.shape["fft"]
-    body = lambda *arrays: exchange_body(band_size, fft_size, *arrays)
+
+    def body(*arrays):
+        return exchange_body(band_size, fft_size, *arrays)
+
     return jax.shard_map(
         body,
         mesh=mesh,

time: 192 us -> 203 us (1.057)
  starting transfers between devices: 30.5 us -> 42 us
  waiting for transfers between devices: 53.7 us -> 64.9 us
  other arithmetic: 8.73 us -> 2.61 us
  blocking collectives: 45.2 us -> 39.4 us
  Pallas kernels: 31.1 us -> 35.4 us
  between operations: 4.74 us -> 0.87 us
    all_to_all x0 -> x3, waiting for transfers between devices: none -> 16.7 us  [exchange_body(): lax.all_to_all(sent, 'fft', split_axis=0, concat_axis=0, tiled=True)]
    ppermute x3, waiting for transfers between devices: 19.5 us -> 2.93 us  [fetch(): return lax.ppermute(value, 'band', pairs)]
    all_to_all x0 -> x3, starting transfers between devices: none -> 10.5 us  [exchange_body(): lax.all_to_all(sent, 'fft', split_axis=0, concat_axis=0, tiled=True)]
    all_to_all x5 -> x4, waiting for transfers between devices: 16.5 us -> 23.1 us  [exchange_body(): lax.all_to_all(spectrum, 'fft', split_axis=0, concat_axis=0, tiled=True)]
    all_to_all x1, blocking collectives: 18.7 us -> 13 us  [exchange_body(): lax.all_to_all(sent, 'fft', split_axis=0, concat_axis=0, tiled=True)]
    all_to_all x2, waiting for transfers between devices: 17.7 us -> 22.1 us  [spread(): rows = lax.all_to_all(rows, 'band', split_axis=0, concat_axis=0, tiled=True)]
    all_to_all x5 -> x4, starting transfers between devices: 17.4 us -> 14 us  [exchange_body(): lax.all_to_all(spectrum, 'fft', split_axis=0, concat_axis=0, tiled=True)]
    integer_pow x2 -> x0, other arithmetic: 2.34 us -> none  [kernel_parts(): first = (frequency(index, extent)[None, :] + qvectors[:, 0:1]) ** 2]
  transfers between devices with their start and end apart: 10 -> 12, of which waited for: 6 -> 11; matrix products, arithmetic and copies ran while one was open for 6% -> 2% of each run, Pallas kernels for 15% -> 12%
where the time goes in v1:
time: 203 us; the launch traced here: 202 us
  waiting for transfers between devices  64.9 us (32%)
  starting transfers between devices  42 us (21%)
  blocking collectives  39.4 us (19%)
  Pallas kernels  35.4 us (17%)
  local copies, waits for them, and re-layouts  12 us (6%)
  matrix products  4.46 us (2%)
  other arithmetic  2.61 us (1%)
    all_to_all x4, waiting for transfers between devices, exchange_body(): lax.all_to_all(spectrum, 'fft', split_axis=0, concat_axis=0, tiled=True)  23.1 us
    all_to_all x2, waiting for transfers between devices, spread(): rows = lax.all_to_all(rows, 'band', split_axis=0, concat_axis=0, tiled=True)  22.1 us
    all_to_all x1, blocking collectives, exchange_body(): lax.all_to_all(projector, 'band', split_axis=0, concat_axis=0, tiled=True)  17.1 us
    all_to_all x3, waiting for transfers between devices, exchange_body(): lax.all_to_all(sent, 'fft', split_axis=0, concat_axis=0, tiled=True)  16.7 us
    all_to_all x4, starting transfers between devices, exchange_body(): lax.all_to_all(spectrum, 'fft', split_axis=0, concat_axis=0, tiled=True)  14 us
    all_to_all x1, blocking collectives, exchange_body(): lax.all_to_all(sent, 'fft', split_axis=0, concat_axis=0, tiled=True)  13 us
    pallas_call x4, Pallas kernels, forward_call(): pl.pallas_call(forward_kernel, grid=(bands, fields, slab // step), in_spe...  12.6 us
    pallas_call x4, Pallas kernels, inverse_call(): pl.pallas_call(body, grid=(bands, slab // step, fields), in_specs=[pl.Blo...  11.6 us
  transfers between devices with their start and end apart: 12, of which 11 were waited for; matrix products, arithmetic and copies ran while one was open for 2% of the time, Pallas kernels for 12%

profile of v1, /device:TPU:0, one launch (start us, length us, event | category | flops | bytes accessed | tf_op | source)
XLA Modules:
  0.0 201.6 jit_solution(9075384247731781662)
XLA Ops:
  0.6 3.1 %collective-permute-start.2 = (f32[1,16,64,128]{3,2,1,0:T(8,128)}, f32[1,16,64,128]{3,2,1,0:T(8,128)S(1)}, u32[]{:S(2)}, u32[]{:S(2)}) collective-permute-start(f32[1,16,64,128]{3,2,1,0:T(8,128)} %refs_1_.1), channel_id=1, source_target_pairs={{4,0},{0,4},{12,8},{8,12},{5,1},{1,5},{13,9},{9,13},{6,2},{2,6},{1... | collective-permute-start | bytes 1572872 | tf_op jit(solution)/shard_map/ppermute | solution.py:375
  3.8 3.1 %forward.4 = f32[4,1,1,2,16,8,128]{6,5,4,3,2,1,0:T(8,128)} custom-call(f32[1,16,64,128]{3,2,1,0:T(8,128)} %orb_ref.7, f32[1,16,64,128]{3,2,1,0:T(8,128)} %refs_1_.1, bf16[2,256,256]{2,1,0:T(8,128)(2,1)} %constant.64.lanes_ref, bf16[64,192]{1,0:T(8,128)(2,1)} %constant.52.clone.rows_ref, f32[2,32,128]{2,1,0:T(8,128)} %constant.53.clone.twid_ref), custom_call_target="tpu_custom_call" | custom-call | flops 1000000000 | bytes 1572864 | tf_op jit(solution)/shard_map/forward/pallas_call | solution.py:237
  6.9 3.5 %all-to-all-start = ((f32[4,1,1,2,16,8,128]{6,5,4,3,2,1,0:T(8,128)}), f32[4,1,1,2,16,8,128]{6,5,4,3,2,1,0:T(8,128)S(1)}, u32[]{:S(2)}, u32[]{:S(2)}) async-start(f32[4,1,1,2,16,8,128]{6,5,4,3,2,1,0:T(8,128)} %forward.4), calls=%async_computation | async-start | bytes 1048576 | tf_op jit(solution)/shard_map/all_to_all | solution.py:421
  14.4 4.8 %all-to-all-done.refs_2_ = f32[4,1,1,2,16,8,128]{6,5,4,3,2,1,0:T(8,128)S(1)} async-done(((f32[4,1,1,2,16,8,128]{6,5,4,3,2,1,0:T(8,128)}), f32[4,1,1,2,16,8,128]{6,5,4,3,2,1,0:T(8,128)S(1)}, u32[]{:S(2)}, u32[]{:S(2)}) %all-to-all-start) | async-done | bytes 524320 | tf_op jit(solution)/shard_map/all_to_all | solution.py:421
  22.3 3.6 %all-to-all-start.2 = ((f32[4,1,1,2,16,8,128]{6,5,4,3,2,1,0:T(8,128)}), f32[4,1,1,2,16,8,128]{6,5,4,3,2,1,0:T(8,128)S(1)}, u32[]{:S(2)}, u32[]{:S(2)}) async-start(f32[4,1,1,2,16,8,128]{6,5,4,3,2,1,0:T(8,128)} %middle.4), calls=%async_computation.2 | async-start | bytes 1048576 | tf_op jit(solution)/shard_map/all_to_all | solution.py:427
  25.9 2.7 %collective-permute-start = (f32[1,16,64,128]{3,2,1,0:T(8,128)S(1)}, f32[1,16,64,128]{3,2,1,0:T(8,128)S(1)}, u32[]{:S(2)}, u32[]{:S(2)}) collective-permute-start(f32[1,16,64,128]{3,2,1,0:T(8,128)S(1)} %copy-done.9), channel_id=1, source_target_pairs={{8,0},{12,4},{0,8},{4,12},{9,1},{13,5},{1,9},{5,13},{10,2},{14,6},... | collective-permute-start | bytes 1572872 | tf_op jit(solution)/shard_map/ppermute | solution.py:375
  29.3 3.1 %forward.5 = f32[4,1,1,2,16,8,128]{6,5,4,3,2,1,0:T(8,128)} custom-call(f32[1,16,64,128]{3,2,1,0:T(8,128)} %orb_ref.7, f32[1,16,64,128]{3,2,1,0:T(8,128)} %copy-done.11, bf16[2,256,256]{2,1,0:T(8,128)(2,1)} %constant.64.lanes_ref, bf16[64,192]{1,0:T(8,128)(2,1)} %constant.52.clone.rows_ref, f32[2,32,128]{2,1,0:T(8,128)} %constant.53.clone.twid_ref), custom_call_target="tpu_custom_call" | custom-call | flops 1000000000 | bytes 1572864 | tf_op jit(solution)/shard_map/forward/pallas_call | solution.py:237
  34.7 3.5 %all-to-all-start.1 = ((f32[4,1,1,2,16,8,128]{6,5,4,3,2,1,0:T(8,128)}), f32[4,1,1,2,16,8,128]{6,5,4,3,2,1,0:T(8,128)S(1)}, u32[]{:S(2)}, u32[]{:S(2)}) async-start(f32[4,1,1,2,16,8,128]{6,5,4,3,2,1,0:T(8,128)} %forward.5), calls=%async_computation.1 | async-start | bytes 1048576 | tf_op jit(solution)/shard_map/all_to_all | solution.py:421
  38.2 2.9 %inverse.4.refs_2_ = f32[1,16,64,128]{3,2,1,0:T(8,128)} custom-call(f32[4,1,1,2,16,8,128]{6,5,4,3,2,1,0:T(8,128)} %copy-done.3, f32[1,16,64,128]{3,2,1,0:T(8,128)} %refs_1_.1, bf16[2,256,256]{2,1,0:T(8,128)(2,1)} %constant.67.refs_2_.refs_3_, bf16[64,192]{1,0:T(8,128)(2,1)} %constant.56.clone.refs_3_.refs_4_, f32[2,32,128]{2,1,0:T(8,128)} %constant.57.clone.refs_4_.refs_5_), custom_call_target="tpu_custom_call" | custom-call | flops 1000000000 | bytes 1572864 | tf_op jit(solution)/shard_map/inverse/pallas_call | solution.py:285
  41.0 5.9 %all-to-all-done.1.refs_2_ = f32[4,1,1,2,16,8,128]{6,5,4,3,2,1,0:T(8,128)S(1)} async-done(((f32[4,1,1,2,16,8,128]{6,5,4,3,2,1,0:T(8,128)}), f32[4,1,1,2,16,8,128]{6,5,4,3,2,1,0:T(8,128)S(1)}, u32[]{:S(2)}, u32[]{:S(2)}) %all-to-all-start.1) | async-done | bytes 524320 | tf_op jit(solution)/shard_map/all_to_all | solution.py:421
  52.9 3.1 %forward.6 = f32[4,1,1,2,16,8,128]{6,5,4,3,2,1,0:T(8,128)} custom-call(f32[1,16,64,128]{3,2,1,0:T(8,128)} %orb_ref.7, f32[1,16,64,128]{3,2,1,0:T(8,128)} %copy-done.12, bf16[2,256,256]{2,1,0:T(8,128)(2,1)} %constant.64.lanes_ref, bf16[64,192]{1,0:T(8,128)(2,1)} %constant.52.clone.rows_ref, f32[2,32,128]{2,1,0:T(8,128)} %constant.53.clone.twid_ref), custom_call_target="tpu_custom_call" | custom-call | flops 1000000000 | bytes 1572864 | tf_op jit(solution)/shard_map/forward/pallas_call | solution.py:237
  56.1 3.6 %all-to-all-start.3 = ((f32[4,1,1,2,16,8,128]{6,5,4,3,2,1,0:T(8,128)}), f32[4,1,1,2,16,8,128]{6,5,4,3,2,1,0:T(8,128)S(1)}, u32[]{:S(2)}, u32[]{:S(2)}) async-start(f32[4,1,1,2,16,8,128]{6,5,4,3,2,1,0:T(8,128)} %forward.6), calls=%async_computation.3 | async-start | bytes 1048576 | tf_op jit(solution)/shard_map/all_to_all | solution.py:421
  59.7 2.7 %collective-permute-start.1 = (f32[1,16,64,128]{3,2,1,0:T(8,128)S(1)}, f32[1,16,64,128]{3,2,1,0:T(8,128)S(1)}, u32[]{:S(2)}, u32[]{:S(2)}) collective-permute-start(f32[1,16,64,128]{3,2,1,0:T(8,128)S(1)} %copy-done.10), channel_id=1, source_target_pairs={{12,0},{8,4},{4,8},{0,12},{13,1},{9,5},{5,9},{1,13},{14,2},{10,6},... | collective-permute-start | bytes 1572872 | tf_op jit(solution)/shard_map/ppermute | solution.py:375
  62.4 6.1 %all-to-all-done.3.refs_2_ = f32[4,1,1,2,16,8,128]{6,5,4,3,2,1,0:T(8,128)S(1)} async-done(((f32[4,1,1,2,16,8,128]{6,5,4,3,2,1,0:T(8,128)}), f32[4,1,1,2,16,8,128]{6,5,4,3,2,1,0:T(8,128)S(1)}, u32[]{:S(2)}, u32[]{:S(2)}) %all-to-all-start.3) | async-done | bytes 524320 | tf_op jit(solution)/shard_map/all_to_all | solution.py:421
  69.3 3.5 %all-to-all-start.4 = ((f32[4,1,1,2,16,8,128]{6,5,4,3,2,1,0:T(8,128)}), f32[4,1,1,2,16,8,128]{6,5,4,3,2,1,0:T(8,128)S(1)}, u32[]{:S(2)}, u32[]{:S(2)}) async-start(f32[4,1,1,2,16,8,128]{6,5,4,3,2,1,0:T(8,128)} %middle.5), calls=%async_computation.4 | async-start | bytes 1048576 | tf_op jit(solution)/shard_map/all_to_all | solution.py:427
  75.9 5.6 %all-to-all-done.4.refs_0_ = f32[4,1,1,2,16,8,128]{6,5,4,3,2,1,0:T(8,128)S(1)} async-done(((f32[4,1,1,2,16,8,128]{6,5,4,3,2,1,0:T(8,128)}), f32[4,1,1,2,16,8,128]{6,5,4,3,2,1,0:T(8,128)S(1)}, u32[]{:S(2)}, u32[]{:S(2)}) %all-to-all-start.4) | async-done | bytes 524320 | tf_op jit(solution)/shard_map/all_to_all | solution.py:427
  82.3 2.9 %inverse.5.refs_2_ = f32[1,16,64,128]{3,2,1,0:T(8,128)} custom-call(f32[4,1,1,2,16,8,128]{6,5,4,3,2,1,0:T(8,128)} %copy-done.6, f32[1,16,64,128]{3,2,1,0:T(8,128)} %copy-done.11, f32[1,16,64,128]{3,2,1,0:T(8,128)} %inverse.4.refs_2_, bf16[2,256,256]{2,1,0:T(8,128)(2,1)} %constant.67.refs_2_.refs_3_, bf16[64,192]{1,0:T(8,128)(2,1)} %constant.56.clone.refs_3_.refs_4_, ...), custom_call_target="tpu_custom_call" | custom-call | flops 1000000000 | bytes 1572864 | tf_op jit(solution)/shard_map/inverse/pallas_call | solution.py:285
  85.3 3.2 %forward.7 = f32[4,1,1,2,16,8,128]{6,5,4,3,2,1,0:T(8,128)} custom-call(f32[1,16,64,128]{3,2,1,0:T(8,128)} %orb_ref.7, f32[1,16,64,128]{3,2,1,0:T(8,128)} %copy-done.13, bf16[2,256,256]{2,1,0:T(8,128)(2,1)} %constant.64.lanes_ref, bf16[64,192]{1,0:T(8,128)(2,1)} %constant.52.clone.rows_ref, f32[2,32,128]{2,1,0:T(8,128)} %constant.53.clone.twid_ref), custom_call_target="tpu_custom_call" | custom-call | flops 1000000000 | bytes 1572864 | tf_op jit(solution)/shard_map/forward/pallas_call | solution.py:237
  88.4 13.0 %all_to_all.60.refs_2_ = f32[4,1,1,2,16,8,128]{6,5,4,3,2,1,0:T(8,128)} all-to-all(f32[4,1,1,2,16,8,128]{6,5,4,3,2,1,0:T(8,128)} %forward.7), channel_id=1, replica_groups=mesh['kgrp'=2,'band'=4,'fft'=4] {'fft'}, dimensions={0} | all-to-all | bytes 1048576 | tf_op jit(solution)/shard_map/all_to_all | solution.py:421
  101.4 3.5 %all-to-all-start.7 = ((f32[4,1,1,2,16,8,128]{6,5,4,3,2,1,0:T(8,128)}), f32[4,1,1,2,16,8,128]{6,5,4,3,2,1,0:T(8,128)S(1)}, u32[]{:S(2)}, u32[]{:S(2)}) async-start(f32[4,1,1,2,16,8,128]{6,5,4,3,2,1,0:T(8,128)} %middle.6), calls=%async_computation.7 | async-start | bytes 1048576 | tf_op jit(solution)/shard_map/all_to_all | solution.py:427
  107.2 6.5 %all-to-all-done.7.refs_0_ = f32[4,1,1,2,16,8,128]{6,5,4,3,2,1,0:T(8,128)S(1)} async-done(((f32[4,1,1,2,16,8,128]{6,5,4,3,2,1,0:T(8,128)}), f32[4,1,1,2,16,8,128]{6,5,4,3,2,1,0:T(8,128)S(1)}, u32[]{:S(2)}, u32[]{:S(2)}) %all-to-all-start.7) | async-done | bytes 524320 | tf_op jit(solution)/shard_map/all_to_all | solution.py:427
  114.5 3.5 %all-to-all-start.6 = ((f32[4,1,1,2,16,8,128]{6,5,4,3,2,1,0:T(8,128)}), f32[4,1,1,2,16,8,128]{6,5,4,3,2,1,0:T(8,128)S(1)}, u32[]{:S(2)}, u32[]{:S(2)}) async-start(f32[4,1,1,2,16,8,128]{6,5,4,3,2,1,0:T(8,128)} %middle.7), calls=%async_computation.6 | async-start | bytes 1048576 | tf_op jit(solution)/shard_map/all_to_all | solution.py:427
  118.0 8.8 %all-to-all-done.6.refs_0_ = f32[4,1,1,2,16,8,128]{6,5,4,3,2,1,0:T(8,128)S(1)} async-done(((f32[4,1,1,2,16,8,128]{6,5,4,3,2,1,0:T(8,128)}), f32[4,1,1,2,16,8,128]{6,5,4,3,2,1,0:T(8,128)S(1)}, u32[]{:S(2)}, u32[]{:S(2)}) %all-to-all-start.6) | async-done | bytes 524320 | tf_op jit(solution)/shard_map/all_to_all | solution.py:427
  127.6 5.5 %all-to-all-start.9 = ((f32[4,1,256,128]{3,2,1,0:T(8,128)}), f32[4,1,256,128]{3,2,1,0:T(8,128)S(1)}, u32[]{:S(2)}, u32[]{:S(2)}) async-start(f32[4,1,256,128]{3,2,1,0:T(8,128)} %bitcast.10), calls=%async_computation.9 | async-start | bytes 1048576 | tf_op jit(solution)/shard_map/all_to_all | solution.py:394
  133.0 2.9 %inverse.6.refs_2_ = f32[1,16,64,128]{3,2,1,0:T(8,128)} custom-call(f32[4,1,1,2,16,8,128]{6,5,4,3,2,1,0:T(8,128)} %copy-done.2, f32[1,16,64,128]{3,2,1,0:T(8,128)} %copy-done.12, f32[1,16,64,128]{3,2,1,0:T(8,128)} %inverse.5.refs_2_, bf16[2,256,256]{2,1,0:T(8,128)(2,1)} %constant.67.refs_2_.refs_3_, bf16[64,192]{1,0:T(8,128)(2,1)} %constant.56.clone.refs_3_.refs_4_, ...), custom_call_target="tpu_custom_call" | custom-call | flops 1000000000 | bytes 1572864 | tf_op jit(solution)/shard_map/inverse/pallas_call | solution.py:285
  136.0 2.9 %inverse.7 = f32[1,16,64,128]{3,2,1,0:T(8,128)} custom-call(f32[4,1,1,2,16,8,128]{6,5,4,3,2,1,0:T(8,128)} %copy-done.4, f32[1,16,64,128]{3,2,1,0:T(8,128)} %copy-done.13, f32[1,16,64,128]{3,2,1,0:T(8,128)} %inverse.6.refs_2_, bf16[2,256,256]{2,1,0:T(8,128)(2,1)} %constant.67.refs_2_.refs_3_, bf16[64,192]{1,0:T(8,128)(2,1)} %constant.56.clone.refs_3_.refs_4_, ...), custom_call_target="tpu_custom_call" | custom-call | flops 1000000000 | bytes 1572864 | tf_op jit(solution)/shard_map/inverse/pallas_call | solution.py:285
  138.9 8.3 %all-to-all-done.9 = f32[4,1,256,128]{3,2,1,0:T(8,128)S(1)} async-done(((f32[4,1,256,128]{3,2,1,0:T(8,128)}), f32[4,1,256,128]{3,2,1,0:T(8,128)S(1)}, u32[]{:S(2)}, u32[]{:S(2)}) %all-to-all-start.9) | async-done | bytes 524320 | tf_op jit(solution)/shard_map/all_to_all | solution.py:394
  147.2 3.5 %all-to-all-start.8 = ((f32[4,1,256,128]{3,2,1,0:T(8,128)}), f32[4,1,256,128]{3,2,1,0:T(8,128)S(1)}, u32[]{:S(2)}, u32[]{:S(2)}) async-start(f32[4,1,256,128]{3,2,1,0:T(8,128)} %bitcast.39), calls=%async_computation.8 | async-start | bytes 1048576 | tf_op jit(solution)/shard_map/all_to_all | solution.py:394
  150.9 13.8 %all-to-all-done.8 = f32[4,1,256,128]{3,2,1,0:T(8,128)S(1)} async-done(((f32[4,1,256,128]{3,2,1,0:T(8,128)}), f32[4,1,256,128]{3,2,1,0:T(8,128)S(1)}, u32[]{:S(2)}, u32[]{:S(2)}) %all-to-all-start.8) | async-done | bytes 524320 | tf_op jit(solution)/shard_map/all_to_all | solution.py:394
  165.7 3.0 %convolution_bitcast_fusion.1 = f32[2,4,4]{1,2,0:T(4,128)S(1)} fusion(f32[2,4,32768]{2,1,0:T(4,128)S(1)} %constant_dynamic-update-slice_fusion, f32[4,32768,1]{1,0,2:T(4,128)S(1)} %reshape.273), kind=kOutput, calls=%fused_computation.3 | convolution fusion | flops 6291456 | bytes 1572992 | tf_op jit(solution)/shard_map/ik,cjk->cij/dot_general | solution.py:439
  168.9 9.3 %all_to_all.61 = f32[16,1,128]{2,1,0:T(1,128)S(1)} all-to-all(f32[16,1,128]{2,1,0:T(1,128)S(1)} %reshape.279), channel_id=1, replica_groups=mesh['kgrp'=2,'band'=4,'fft'=4] {'band','fft'}, dimensions={0} | all-to-all | bytes 16384 | tf_op jit(solution)/shard_map/all_to_all | solution.py:366
  183.6 17.1 %all_to_all.62 = f32[4,1,256,128]{3,2,1,0:T(8,128)S(1)} all-to-all(f32[4,1,256,128]{3,2,1,0:T(8,128)S(1)} %bitcast.37), channel_id=1, replica_groups=mesh['kgrp'=2,'band'=4,'fft'=4] {'band'}, dimensions={0} | all-to-all | bytes 1048576 | tf_op jit(solution)/shard_map/all_to_all | solution.py:447
  (72 shorter events, 32.4 us)
Async XLA Ops:
  0.6 9.9 %copy-start = (s32[4]{0:T(128)S(1)}, s32[4]{0:T(128)}, u32[]{:S(2)}) copy-start(s32[4]{0:T(128)} %param.15) | copy-start | bytes 52
  0.6 27.9 %collective-permute-start.2 = (f32[1,16,64,128]{3,2,1,0:T(8,128)}, f32[1,16,64,128]{3,2,1,0:T(8,128)S(1)}, u32[]{:S(2)}, u32[]{:S(2)}) collective-permute-start(f32[1,16,64,128]{3,2,1,0:T(8,128)} %refs_1_.1), channel_id=1, source_target_pairs={{4,0},{0,4},{12,8},{8,12},{5,1},{1,5},{13,9},{9,13},{6,2},{2,6},{1... | collective-permute-start | bytes 1572872 | tf_op jit(solution)/shard_map/ppermute | solution.py:375
  6.9 12.3 %all-to-all-start = ((f32[4,1,1,2,16,8,128]{6,5,4,3,2,1,0:T(8,128)}), f32[4,1,1,2,16,8,128]{6,5,4,3,2,1,0:T(8,128)S(1)}, u32[]{:S(2)}, u32[]{:S(2)}) async-start(f32[4,1,1,2,16,8,128]{6,5,4,3,2,1,0:T(8,128)} %forward.4), calls=%async_computation | async-start | bytes 1048576 | tf_op jit(solution)/shard_map/all_to_all | solution.py:421
  11.1 0.7 copy-start.8
  19.2 0.8 copy-start.1
  22.3 3.6 %copy-start.9 = (f32[1,16,64,128]{3,2,1,0:T(8,128)S(1)}, f32[1,16,64,128]{3,2,1,0:T(8,128)}, u32[]{:S(2)}) copy-start(f32[1,16,64,128]{3,2,1,0:T(8,128)} %refs_1_.1) | copy-start | bytes 1572868
  22.3 12.4 %all-to-all-start.2 = ((f32[4,1,1,2,16,8,128]{6,5,4,3,2,1,0:T(8,128)}), f32[4,1,1,2,16,8,128]{6,5,4,3,2,1,0:T(8,128)S(1)}, u32[]{:S(2)}, u32[]{:S(2)}) async-start(f32[4,1,1,2,16,8,128]{6,5,4,3,2,1,0:T(8,128)} %middle.4), calls=%async_computation.2 | async-start | bytes 1048576 | tf_op jit(solution)/shard_map/all_to_all | solution.py:427
  25.9 26.3 %collective-permute-start = (f32[1,16,64,128]{3,2,1,0:T(8,128)S(1)}, f32[1,16,64,128]{3,2,1,0:T(8,128)S(1)}, u32[]{:S(2)}, u32[]{:S(2)}) collective-permute-start(f32[1,16,64,128]{3,2,1,0:T(8,128)S(1)} %copy-done.9), channel_id=1, source_target_pairs={{8,0},{12,4},{0,8},{4,12},{9,1},{13,5},{1,9},{5,13},{10,2},{14,6},... | collective-permute-start | bytes 1572872 | tf_op jit(solution)/shard_map/ppermute | solution.py:375
  28.5 0.8 copy-start.11
  34.7 3.5 %copy-start.3 = (f32[4,1,1,2,16,8,128]{6,5,4,3,2,1,0:T(8,128)}, f32[4,1,1,2,16,8,128]{6,5,4,3,2,1,0:T(8,128)S(1)}, u32[]{:S(2)}) copy-start(f32[4,1,1,2,16,8,128]{6,5,4,3,2,1,0:T(8,128)S(1)} %all-to-all-done.2.refs_0_) | copy-start | bytes 1572868
  34.7 12.3 %all-to-all-start.1 = ((f32[4,1,1,2,16,8,128]{6,5,4,3,2,1,0:T(8,128)}), f32[4,1,1,2,16,8,128]{6,5,4,3,2,1,0:T(8,128)S(1)}, u32[]{:S(2)}, u32[]{:S(2)}) async-start(f32[4,1,1,2,16,8,128]{6,5,4,3,2,1,0:T(8,128)} %forward.5), calls=%async_computation.1 | async-start | bytes 1048576 | tf_op jit(solution)/shard_map/all_to_all | solution.py:421
  46.9 0.8 copy-start.7
  52.1 0.8 copy-start.12
  56.1 3.6 %copy-start.10 = (f32[1,16,64,128]{3,2,1,0:T(8,128)S(1)}, f32[1,16,64,128]{3,2,1,0:T(8,128)}, u32[]{:S(2)}) copy-start(f32[1,16,64,128]{3,2,1,0:T(8,128)} %refs_1_.1) | copy-start | bytes 1572868
  56.1 12.4 %all-to-all-start.3 = ((f32[4,1,1,2,16,8,128]{6,5,4,3,2,1,0:T(8,128)}), f32[4,1,1,2,16,8,128]{6,5,4,3,2,1,0:T(8,128)S(1)}, u32[]{:S(2)}, u32[]{:S(2)}) async-start(f32[4,1,1,2,16,8,128]{6,5,4,3,2,1,0:T(8,128)} %forward.6), calls=%async_computation.3 | async-start | bytes 1048576 | tf_op jit(solution)/shard_map/all_to_all | solution.py:421
  59.7 16.2 %collective-permute-start.1 = (f32[1,16,64,128]{3,2,1,0:T(8,128)S(1)}, f32[1,16,64,128]{3,2,1,0:T(8,128)S(1)}, u32[]{:S(2)}, u32[]{:S(2)}) collective-permute-start(f32[1,16,64,128]{3,2,1,0:T(8,128)S(1)} %copy-done.10), channel_id=1, source_target_pairs={{12,0},{8,4},{4,8},{0,12},{13,1},{9,5},{5,9},{1,13},{14,2},{10,6},... | collective-permute-start | bytes 1572872 | tf_op jit(solution)/shard_map/ppermute | solution.py:375
  68.5 0.8 copy-start.5
  69.3 12.3 %all-to-all-start.4 = ((f32[4,1,1,2,16,8,128]{6,5,4,3,2,1,0:T(8,128)}), f32[4,1,1,2,16,8,128]{6,5,4,3,2,1,0:T(8,128)S(1)}, u32[]{:S(2)}, u32[]{:S(2)}) async-start(f32[4,1,1,2,16,8,128]{6,5,4,3,2,1,0:T(8,128)} %middle.5), calls=%async_computation.4 | async-start | bytes 1048576 | tf_op jit(solution)/shard_map/all_to_all | solution.py:427
  75.9 9.4 %copy-start.13 = (f32[1,16,64,128]{3,2,1,0:T(8,128)}, f32[1,16,64,128]{3,2,1,0:T(8,128)S(1)}, u32[]{:S(2)}) copy-start(f32[1,16,64,128]{3,2,1,0:T(8,128)S(1)} %collective-permute-done.1.part_ref.refs_1_) | copy-start | bytes 1572868
  81.5 0.8 copy-start.6
  101.4 12.3 %all-to-all-start.7 = ((f32[4,1,1,2,16,8,128]{6,5,4,3,2,1,0:T(8,128)}), f32[4,1,1,2,16,8,128]{6,5,4,3,2,1,0:T(8,128)S(1)}, u32[]{:S(2)}, u32[]{:S(2)}) async-start(f32[4,1,1,2,16,8,128]{6,5,4,3,2,1,0:T(8,128)} %middle.6), calls=%async_computation.7 | async-start | bytes 1048576 | tf_op jit(solution)/shard_map/all_to_all | solution.py:427
  113.7 0.8 copy-start.2
  114.5 12.3 %all-to-all-start.6 = ((f32[4,1,1,2,16,8,128]{6,5,4,3,2,1,0:T(8,128)}), f32[4,1,1,2,16,8,128]{6,5,4,3,2,1,0:T(8,128)S(1)}, u32[]{:S(2)}, u32[]{:S(2)}) async-start(f32[4,1,1,2,16,8,128]{6,5,4,3,2,1,0:T(8,128)} %middle.7), calls=%async_computation.6 | async-start | bytes 1048576 | tf_op jit(solution)/shard_map/all_to_all | solution.py:427
  126.7 0.8 copy-start.4
  127.6 19.7 %all-to-all-start.9 = ((f32[4,1,256,128]{3,2,1,0:T(8,128)}), f32[4,1,256,128]{3,2,1,0:T(8,128)S(1)}, u32[]{:S(2)}, u32[]{:S(2)}) async-start(f32[4,1,256,128]{3,2,1,0:T(8,128)} %bitcast.10), calls=%async_computation.9 | async-start | bytes 1048576 | tf_op jit(solution)/shard_map/all_to_all | solution.py:394
  147.2 17.5 %all-to-all-start.8 = ((f32[4,1,256,128]{3,2,1,0:T(8,128)}), f32[4,1,256,128]{3,2,1,0:T(8,128)S(1)}, u32[]{:S(2)}, u32[]{:S(2)}) async-start(f32[4,1,256,128]{3,2,1,0:T(8,128)} %bitcast.39), calls=%async_computation.8 | async-start | bytes 1048576 | tf_op jit(solution)/shard_map/all_to_all | solution.py:394
